TPU v7x, 32 devices: a whole 2x2x4 slice. The times are simulated.
32 devices in a mesh: dp: 8 (over z, x), mp: 4 (over y, core).
Axes of the slice: x: 2, y: 2, z: 4, core: 2. Of those that a mesh axis runs over, the one named last changes fastest.
Arguments:
- queries: bfloat16 [16, 16, 5120], P('dp', None, 'mp')
- key_value_cache: bfloat16 [128, 2, 128, 1024], P('dp', None, None, 'mp'), may hold values from -6 to 6
- slot_tags: int32 [128], P('dp'), may hold values from 0 to 15, as said below
- span_key_value: bfloat16 [16, 2, 16, 1024], P('dp', None, None, 'mp'), may hold values from -6 to 6
- answer_id: int32 [16], P('dp'), may hold values from 0 to 127
- w_cand: bfloat16 [5120, 128], P('mp')
Outputs:
- attended: bfloat16 [16, 16, 5120], P('dp', None, 'mp')
- chain_score: float32 [16], P('dp')
- answer_tally: float32 [1, 128], P(None, 'dp')
Inputs may be any that keep to these rules, and one draw needn't show every extreme that they name: `slot_tags`: among the 16 blocks of any one index of dp, at most 2 belong to the chains o * 2 to o * 2 + 1 of any one o, and for some o every index of dp holds exactly 2 such blocks. A chain may have no cached block.
All inputs are finite; a program needn't handle non-finite values.
Results may differ from a plain program's by a relative error of at most 0.0075.
Values may be sent and summed in bfloat16 or wider, within the bound.
No kernel may reach another device: no remote copies, remote signals or barrier semaphores. Data moves between devices by JAX's collectives and lax.ppermute only.
A program may use at most 128 MiB of HBM per device.

v0:
```python
import jax
import jax.numpy as jnp
from jax import lax
from jax.sharding import PartitionSpec as P

QUERY_HEADS = 40
KEY_VALUE_HEADS = 8
HEAD_SIZE = 128
NCAND = 128
PEER = 2
SAMPLES = 16
big_neg = -1e30


def block_terms(picked, blocks, causal):
    count = picked.shape[0]
    span = picked.shape[1]
    width = blocks.shape[2]
    heads_kv = blocks.shape[3] // HEAD_SIZE
    head_group = QUERY_HEADS // KEY_VALUE_HEADS
    query_rows = picked.reshape(count, span, heads_kv, head_group, HEAD_SIZE)
    lookup_matrix = blocks[:, 0].reshape(count, width, heads_kv, HEAD_SIZE)
    value_rows = blocks[:, 1].reshape(count, width, heads_kv, HEAD_SIZE)
    logit_rows = jnp.einsum(
        "nakgd,nbkd->nkgab", query_rows, lookup_matrix, preferred_element_type=jnp.float32
    ) * HEAD_SIZE ** (-0.5)
    if causal:
        allowed = jnp.arange(span)[:, None] >= jnp.arange(width)[None, :]
        logit_rows = jnp.where(allowed, logit_rows, big_neg)
    peaks = jnp.max(logit_rows, axis=-1)
    weights = jnp.exp(logit_rows - peaks[..., None])
    totals = jnp.sum(weights, axis=-1)
    summed_scores = jnp.einsum(
        "nkgab,nbkd->nkgad",
        weights.astype(jnp.bfloat16),
        value_rows,
        preferred_element_type=jnp.float32,
    )
    return (peaks, totals, summed_scores)


def merge_items(peaks, totals, summed_scores, member):
    member_f = member.astype(jnp.float32)
    masked = jnp.where(member[:, :, None, None, None], peaks[:, None], big_neg)
    chain_peak = jnp.max(masked, axis=0)
    item_peak = jnp.einsum("nc,ckga->nkga", member_f, chain_peak, precision=lax.Precision.HIGHEST)
    present = jnp.any(member, axis=1)
    factor = jnp.where(present[:, None, None, None], jnp.exp(peaks - item_peak), 0.0)
    chain_total = jnp.einsum(
        "nc,nkga->ckga", member_f, totals * factor, precision=lax.Precision.HIGHEST
    )
    chain_sum = jnp.einsum(
        "nc,nkgad->ckgad",
        member_f,
        summed_scores * factor[..., None],
        precision=lax.Precision.HIGHEST,
    )
    return (chain_peak, chain_total, chain_sum)


def fold_pair(first, second):
    overall = jnp.maximum(first[0], second[0])
    left = jnp.exp(first[0] - overall)
    right = jnp.exp(second[0] - overall)
    total = first[1] * left + second[1] * right
    summed_scores = first[2] * left[..., None] + second[2] * right[..., None]
    return (overall, total, summed_scores)


def per_device(queries, key_value_cache, slot_tags, span_key_value, answer_id, w_cand):
    accelerator_roster = lax.axis_size("dp")
    position = lax.axis_index("dp")
    chains_here = queries.shape[0]
    features = queries.shape[2]
    slots_here = slot_tags.shape[0]
    owner_index = slot_tags // chains_here
    chain_local = slot_tags % chains_here
    owner_hot = (
        owner_index[:, None] == jnp.arange(accelerator_roster, dtype=jnp.int32)[None, :]
    ).astype(jnp.int32)
    running = jnp.cumsum(owner_hot, axis=0) - 1
    rank_in = jnp.sum(owner_hot * running, axis=1)
    target = owner_index * PEER + rank_in
    places_all = accelerator_roster * PEER
    hit = (target[:, None] == jnp.arange(places_all, dtype=jnp.int32)[None, :]).astype(jnp.int32)
    source_row = jnp.sum(hit * jnp.arange(slots_here, dtype=jnp.int32)[:, None], axis=0)
    is_filled = jnp.sum(hit, axis=0) > 0
    send_chain = jnp.where(is_filled, jnp.sum(hit * chain_local[:, None], axis=0), chains_here)
    send_blocks = key_value_cache[source_row].reshape(
        (accelerator_roster, PEER) + key_value_cache.shape[1:]
    )
    send_chain = send_chain.reshape(accelerator_roster, PEER)
    blocks = lax.all_to_all(send_blocks, "dp", split_axis=0, concat_axis=0, tiled=True)
    places = lax.all_to_all(send_chain, "dp", split_axis=0, concat_axis=0, tiled=True)
    count = places.shape[0] * places.shape[1]
    flat_places = places.reshape(count)
    picked = queries[jnp.clip(flat_places, 0, chains_here - 1)]
    peaks, totals, summed_scores = block_terms(
        picked, blocks.reshape((count,) + blocks.shape[2:]), False
    )
    lead = places.shape
    peaks, totals, summed_scores, places = (
        peaks.reshape(lead + peaks.shape[1:]),
        totals.reshape(lead + totals.shape[1:]),
        summed_scores.reshape(lead + summed_scores.shape[1:]),
        places,
    )
    count = places.shape[0] * places.shape[1]
    member = places.reshape(count)[:, None] == jnp.arange(chains_here, dtype=jnp.int32)[None, :]
    remote = merge_items(
        peaks.reshape((count,) + peaks.shape[2:]),
        totals.reshape((count,) + totals.shape[2:]),
        summed_scores.reshape((count,) + summed_scores.shape[2:]),
        member,
    )
    own_span = block_terms(queries, span_key_value, True)
    final_peak, final_total, final_sum = fold_pair(own_span, remote)
    output = final_sum / final_total[..., None]
    output = jnp.transpose(output, (0, 3, 1, 2, 4)).reshape(chains_here, queries.shape[1], features)
    attended = output.astype(jnp.bfloat16)
    span = queries.shape[1]
    partial_logits = jnp.dot(
        attended.reshape(chains_here * span, features), w_cand, preferred_element_type=jnp.float32
    )
    logit_rows = lax.psum(partial_logits, "mp").reshape(chains_here, span, NCAND)
    top_logit = jnp.max(logit_rows, axis=-1, keepdims=True)
    log_norm = top_logit[..., 0] + jnp.log(jnp.sum(jnp.exp(logit_rows - top_logit), axis=-1))
    answer_hot = (answer_id[:, None] == jnp.arange(NCAND, dtype=jnp.int32)[None, :]).astype(
        jnp.float32
    )
    chosen_logit = jnp.sum(logit_rows * answer_hot[:, None, :], axis=-1)
    chain_score = jnp.mean(chosen_logit - log_norm, axis=-1)
    prompt_count = accelerator_roster * chains_here // SAMPLES
    global_chain = position * chains_here + jnp.arange(chains_here, dtype=jnp.int32)
    prompt_hot = (
        (global_chain // SAMPLES)[:, None] == jnp.arange(prompt_count, dtype=jnp.int32)[None, :]
    ).astype(jnp.float32)
    tally_terms = jnp.dot(
        prompt_hot.T, chain_score[:, None] * answer_hot, precision=lax.Precision.HIGHEST
    )
    answer_tally = lax.psum_scatter(tally_terms, "dp", scatter_dimension=1, tiled=True)
    return (attended, chain_score, answer_tally)


def solution(mesh):
    in_specs = (
        P("dp", None, "mp"),
        P("dp", None, None, "mp"),
        P("dp"),
        P("dp", None, None, "mp"),
        P("dp"),
        P("mp", None),
    )
    out_specs = (P("dp", None, "mp"), P("dp"), P(None, "dp"))
    return jax.shard_map(
        per_device, mesh=mesh, in_specs=in_specs, out_specs=out_specs, check_vma=False
    )
```

profile of v0, /device:TPU:0, one launch (start us, length us, event | category | flops | bytes accessed | tf_op | source)
XLA Modules:
  0.0 165.2 jit_solution(9929074711548436345)
XLA Ops:
  7.2 0.8 and_select_fusion.1
  8.4 0.7 select_n.71
  9.1 7.3 %all-to-all-start = ((s32[8,1,2]{2,1,0:T(1,128)}), s32[8,1,2]{2,1,0:T(1,128)S(1)}, u32[]{:S(2)}, u32[]{:S(2)}) async-start(s32[8,1,2]{2,1,0:T(1,128)} %bitcast.5), calls=%async_computation | async-start | bytes 8192 | tf_op jit(solution)/shard_map/all_to_all | solution.py:94
  16.4 2.0 %gather_fusion = bf16[16,2,128,256]{3,2,1,0:T(8,128)(2,1)} fusion(bf16[16,2,128,256]{3,2,1,0:T(8,128)(2,1)S(1)} %copy-done, s32[1024]{0:T(1024)S(1)} %pad_clamp_fusion.1), kind=kCustom, calls=%fused_computation | custom fusion | bytes 4194368 | tf_op jit(solution)/shard_map/gather | solution.py:89
  18.4 3.9 %copy.89 = bf16[8,2,2,128,256]{3,4,1,2,0:T(8,128)(2,1)} copy(bf16[8,2,2,128,256]{4,3,2,1,0:T(8,128)(2,1)} %bitcast.89) | data formatting | bytes 4194304 | tf_op jit(solution)/shard_map/reshape | solution.py:89
  22.3 0.5 all-to-all-done
  22.8 5.7 %all-to-all-start.1 = ((bf16[8,2,2,128,256]{3,4,1,2,0:T(8,128)(2,1)}), bf16[8,2,2,128,256]{3,4,1,2,0:T(8,128)(2,1)}, u32[]{:S(2)}, u32[]{:S(2)}) async-start(bf16[8,2,2,128,256]{3,4,1,2,0:T(8,128)(2,1)} %copy.89), calls=%async_computation.1 | async-start | bytes 4194304 | tf_op jit(solution)/shard_map/all_to_all | solution.py:93
  28.7 0.3 fusion.64
  29.1 0.5 broadcast.247
  29.6 0.7 fusion.60
  30.4 1.4 gather_fusion.1
  31.8 1.8 %reshape.177 = bf16[16,16,2,5,128]{4,3,2,1,0:T(8,128)(2,1)S(1)} reshape(bf16[16,16,1280]{2,1,0:T(8,128)(2,1)} %gather_fusion.1) | data formatting | bytes 1310720 | tf_op jit(solution)/shard_map/reshape | solution.py:21
  33.7 42.5 %all-to-all-done.1 = bf16[8,2,2,128,256]{3,4,1,2,0:T(8,128)(2,1)} async-done(((bf16[8,2,2,128,256]{3,4,1,2,0:T(8,128)(2,1)}), bf16[8,2,2,128,256]{3,4,1,2,0:T(8,128)(2,1)}, u32[]{:S(2)}, u32[]{:S(2)}) %all-to-all-start.1) | async-done | bytes 2097184 | tf_op jit(solution)/shard_map/all_to_all | solution.py:93
  76.2 1.7 %copy.90 = bf16[8,2,2,128,256]{3,4,1,0,2:T(8,128)(2,1)S(1)} copy(bf16[8,2,2,128,256]{3,4,1,2,0:T(8,128)(2,1)} %all-to-all-done.1) | data formatting | bytes 4194304 | tf_op jit(solution)/shard_map/all_to_all | solution.py:93
  78.2 0.6 fusion.63
  79.2 0.8 fusion.3
  80.0 1.4 convolution_multiply_fusion
  81.5 1.3 fusion.1
  83.0 0.3 fusion.10
  83.6 10.1 %psum.7 = f32[32,128]{1,0:T(8,128)S(1)} all-reduce(f32[32,128]{1,0:T(8,128)S(1)} %fusion.65), channel_id=1, replica_groups=mesh['dp'=8,'mp'=4] {'mp'}, use_global_device_ids=true, to_apply=%region_11.12 | all-reduce | flops 4096 | bytes 32768 | tf_op jit(solution)/shard_map/psum | solution.py:125
  94.3 1.0 convolution_bitcast_fusion.1
  95.2 0.7 convert_element_type.36
  96.0 61.1 %reduce-scatter.4.cloned.1.call-done = f32[16,1]{1,0:T(8,128)} async-done(((f32[128,1]{1,0:T(8,128)}), f32[16,1]{1,0:T(8,128)}) %reduce-scatter.4.cloned.1.call-update) | async-done | bytes 80
  157.1 1.3 copy.124
  (53 shorter events, 2.6 us)
Async XLA Ops:
  7.2 9.2 %copy-start = (bf16[16,2,128,256]{3,2,1,0:T(8,128)(2,1)S(1)}, bf16[16,2,128,256]{3,2,1,0:T(8,128)(2,1)}, u32[]{:S(2)}) copy-start(bf16[16,2,128,256]{3,2,1,0:T(8,128)(2,1)} %param.7) | copy-start | bytes 6291460
  9.1 13.7 %all-to-all-start = ((s32[8,1,2]{2,1,0:T(1,128)}), s32[8,1,2]{2,1,0:T(1,128)S(1)}, u32[]{:S(2)}, u32[]{:S(2)}) async-start(s32[8,1,2]{2,1,0:T(1,128)} %bitcast.5), calls=%async_computation | async-start | bytes 8192 | tf_op jit(solution)/shard_map/all_to_all | solution.py:94
  22.3 6.2 %copy-start.1 = (bf16[2,16,1280]{2,1,0:T(8,128)(2,1)S(1)}, bf16[2,16,1280]{2,1,0:T(8,128)(2,1)}, u32[]{:S(2)}) copy-start(bf16[2,16,1280]{2,1,0:T(8,128)(2,1)} %param.6) | copy-start | bytes 245764
  22.3 6.3 %copy-start.3 = (bf16[2,2,16,256]{3,2,1,0:T(8,128)(2,1)S(1)}, bf16[2,2,16,256]{3,2,1,0:T(8,128)(2,1)}, u32[]{:S(2)}) copy-start(bf16[2,2,16,256]{3,2,1,0:T(8,128)(2,1)} %param.9) | copy-start | bytes 98308
  22.3 6.8 %copy-start.4 = (s32[2]{0:T(128)S(1)}, s32[2]{0:T(128)}, u32[]{:S(2)}) copy-start(s32[2]{0:T(128)} %param.10) | copy-start | bytes 28
  22.8 53.4 %all-to-all-start.1 = ((bf16[8,2,2,128,256]{3,4,1,2,0:T(8,128)(2,1)}), bf16[8,2,2,128,256]{3,4,1,2,0:T(8,128)(2,1)}, u32[]{:S(2)}, u32[]{:S(2)}) async-start(bf16[8,2,2,128,256]{3,4,1,2,0:T(8,128)(2,1)} %copy.89), calls=%async_computation.1 | async-start | bytes 4194304 | tf_op jit(solution)/shard_map/all_to_all | solution.py:93
  28.4 128.6 %reduce-scatter.4.cloned.1.call-start = ((), (), s32[]{:S(2)}) async-start(), calls=%async_computation.3 | async-start | bytes 73728
  81.5 1.9 %copy-start.2 = (bf16[1280,128]{1,0:T(8,128)(2,1)S(1)}, bf16[1280,128]{1,0:T(8,128)(2,1)}, u32[]{:S(2)}) copy-start(bf16[1280,128]{1,0:T(8,128)(2,1)} %param.11) | copy-start | bytes 983044
  94.2 64.1 %copy-start.5 = (f32[2]{0:T(128)}, f32[2]{0:T(128)S(1)}, u32[]{:S(2)}) copy-start(f32[2]{0:T(128)S(1)} %broadcast_multiply_fusion) | copy-start | bytes 28
Sparse Core Ops, SparseCore 0:
  95.4 61.6 reduce-scatter.3
where the time goes:
time: 166 us; the launch traced here: 165 us
  waiting for transfers between devices  104 us (63%)
  local copies, waits for them, and re-layouts  14.9 us (9%)
  between operations  14.3 us (9%)
  starting transfers between devices  13 us (8%)
  blocking collectives  10.1 us (6%)
  matrix products  5.37 us (3%)
  other arithmetic  3.42 us (2%)
    unnamed x2, waiting for transfers between devices  61.1 us
    all_to_all x1, waiting for transfers between devices, per_device(): lax.all_to_all(send_blocks, 'dp', split_axis=0, concat_axis=0, tiled=True)  42.5 us
    psum x1, blocking collectives, per_device(): lax.psum(partial_logits, 'mp').reshape(chains_here, span, NCAND)  10.1 us
    all_to_all x1, starting transfers between devices, per_device(): lax.all_to_all(send_chain, 'dp', split_axis=0, concat_axis=0, tiled=True)  7.28 us
    all_to_all x1, starting transfers between devices, per_device(): lax.all_to_all(send_blocks, 'dp', split_axis=0, concat_axis=0, tiled=True)  5.66 us
    reshape x1, local copies, waits for them, and re-layouts, per_device(): key_value_cache[source_row]  3.92 us
  transfers between devices with their start and end apart: 3, of which 3 were waited for; matrix products, arithmetic and copies ran while one was open for 7% of the time, Pallas kernels for 0%

commit v1 on v0

--- a/solution.py
+++ b/solution.py
@@ -122,7 +122,9 @@
     partial_logits = jnp.dot(
         attended.reshape(chains_here * span, features), w_cand, preferred_element_type=jnp.float32
     )
-    logit_rows = lax.psum(partial_logits, "mp").reshape(chains_here, span, NCAND)
+    logit_rows = jnp.sum(lax.all_gather(partial_logits, "mp"), axis=0).reshape(
+        chains_here, span, NCAND
+    )
     top_logit = jnp.max(logit_rows, axis=-1, keepdims=True)
     log_norm = top_logit[..., 0] + jnp.log(jnp.sum(jnp.exp(logit_rows - top_logit), axis=-1))
     answer_hot = (answer_id[:, None] == jnp.arange(NCAND, dtype=jnp.int32)[None, :]).astype(

time: 166 us -> 161 us (0.970)
  blocking collectives: 10.1 us -> 5.24 us
    psum x1 -> x0, blocking collectives: 10.1 us -> none  [per_device(): lax.psum(partial_logits, 'mp').reshape(chains_here, span, NCAND)]
    all_gather x0 -> x1, blocking collectives: none -> 5.24 us  [per_device(): lax.all_gather(partial_logits, 'mp')]
where the time goes in v1:
time: 161 us; the launch traced here: 160 us
  waiting for transfers between devices  104 us (65%)
  local copies, waits for them, and re-layouts  14.9 us (9%)
  between operations  14.3 us (9%)
  starting transfers between devices  13 us (8%)
  matrix products  5.37 us (3%)
  blocking collectives  5.24 us (3%)
  other arithmetic  3.52 us (2%)
    unnamed x2, waiting for transfers between devices  61 us
    all_to_all x1, waiting for transfers between devices, per_device(): lax.all_to_all(send_blocks, 'dp', split_axis=0, concat_axis=0, tiled=True)  42.5 us
    all_to_all x1, starting transfers between devices, per_device(): lax.all_to_all(send_chain, 'dp', split_axis=0, concat_axis=0, tiled=True)  7.28 us
    all_to_all x1, starting transfers between devices, per_device(): lax.all_to_all(send_blocks, 'dp', split_axis=0, concat_axis=0, tiled=True)  5.66 us
    all_gather x1, blocking collectives, per_device(): lax.all_gather(partial_logits, 'mp')  5.24 us
    reshape x1, local copies, waits for them, and re-layouts, per_device(): key_value_cache[source_row]  3.92 us
  transfers between devices with their start and end apart: 3, of which 3 were waited for; matrix products, arithmetic and copies ran while one was open for 7% of the time, Pallas kernels for 0%

profile of v1, /device:TPU:0, one launch (start us, length us, event | category | flops | bytes accessed | tf_op | source)
XLA Modules:
  0.0 160.3 jit_solution(2322961470429245331)
XLA Ops:
  7.2 0.8 and_select_fusion.1
  8.4 0.7 select_n.71
  9.1 7.3 %all-to-all-start = ((s32[8,1,2]{2,1,0:T(1,128)}), s32[8,1,2]{2,1,0:T(1,128)S(1)}, u32[]{:S(2)}, u32[]{:S(2)}) async-start(s32[8,1,2]{2,1,0:T(1,128)} %bitcast.5), calls=%async_computation | async-start | bytes 8192 | tf_op jit(solution)/shard_map/all_to_all | solution.py:94
  16.4 2.0 %gather_fusion = bf16[16,2,128,256]{3,2,1,0:T(8,128)(2,1)} fusion(bf16[16,2,128,256]{3,2,1,0:T(8,128)(2,1)S(1)} %copy-done, s32[1024]{0:T(1024)S(1)} %pad_clamp_fusion.1), kind=kCustom, calls=%fused_computation | custom fusion | bytes 4194368 | tf_op jit(solution)/shard_map/gather | solution.py:89
  18.4 3.9 %copy.89 = bf16[8,2,2,128,256]{3,4,1,2,0:T(8,128)(2,1)} copy(bf16[8,2,2,128,256]{4,3,2,1,0:T(8,128)(2,1)} %bitcast.87) | data formatting | bytes 4194304 | tf_op jit(solution)/shard_map/reshape | solution.py:89
  22.3 0.5 all-to-all-done
  22.8 5.7 %all-to-all-start.1 = ((bf16[8,2,2,128,256]{3,4,1,2,0:T(8,128)(2,1)}), bf16[8,2,2,128,256]{3,4,1,2,0:T(8,128)(2,1)}, u32[]{:S(2)}, u32[]{:S(2)}) async-start(bf16[8,2,2,128,256]{3,4,1,2,0:T(8,128)(2,1)} %copy.89), calls=%async_computation.1 | async-start | bytes 4194304 | tf_op jit(solution)/shard_map/all_to_all | solution.py:93
  28.7 0.3 fusion.63
  29.1 0.5 broadcast.248
  29.6 0.7 fusion.59
  30.4 1.4 gather_fusion.1
  31.8 1.8 %reshape.184 = bf16[16,16,2,5,128]{4,3,2,1,0:T(8,128)(2,1)S(1)} reshape(bf16[16,16,1280]{2,1,0:T(8,128)(2,1)} %gather_fusion.1) | data formatting | bytes 1310720 | tf_op jit(solution)/shard_map/reshape | solution.py:21
  33.7 42.5 %all-to-all-done.1 = bf16[8,2,2,128,256]{3,4,1,2,0:T(8,128)(2,1)} async-done(((bf16[8,2,2,128,256]{3,4,1,2,0:T(8,128)(2,1)}), bf16[8,2,2,128,256]{3,4,1,2,0:T(8,128)(2,1)}, u32[]{:S(2)}, u32[]{:S(2)}) %all-to-all-start.1) | async-done | bytes 2097184 | tf_op jit(solution)/shard_map/all_to_all | solution.py:93
  76.2 1.7 %copy.90 = bf16[8,2,2,128,256]{3,4,1,0,2:T(8,128)(2,1)S(1)} copy(bf16[8,2,2,128,256]{3,4,1,2,0:T(8,128)(2,1)} %all-to-all-done.1) | data formatting | bytes 4194304 | tf_op jit(solution)/shard_map/all_to_all | solution.py:93
  78.2 0.6 fusion.62
  79.2 0.8 fusion.3
  80.0 1.4 convolution_multiply_fusion
  81.5 1.3 fusion.1
  83.0 0.3 fusion.10
  83.6 5.2 %all-gather = f32[128,128]{1,0:T(8,128)S(1)} all-gather(f32[32,128]{1,0:T(8,128)S(1)} %fusion.64), channel_id=2, replica_groups=mesh['dp'=8,'mp'=4] {'mp'}, dimensions={0}, use_global_device_ids=true | all-gather | bytes 81920 | tf_op jit(solution)/shard_map/all_gather | solution.py:125
  89.5 1.0 convolution_bitcast_fusion.1
  90.4 0.7 convert_element_type.36
  91.2 60.9 %reduce-scatter.4.cloned.1.call-done = f32[16,1]{1,0:T(8,128)} async-done(((f32[128,1]{1,0:T(8,128)}), f32[16,1]{1,0:T(8,128)}) %reduce-scatter.4.cloned.1.call-update) | async-done | bytes 80
  152.1 1.3 copy.124
  (55 shorter events, 2.7 us)
Async XLA Ops:
  7.2 9.2 %copy-start = (bf16[16,2,128,256]{3,2,1,0:T(8,128)(2,1)S(1)}, bf16[16,2,128,256]{3,2,1,0:T(8,128)(2,1)}, u32[]{:S(2)}) copy-start(bf16[16,2,128,256]{3,2,1,0:T(8,128)(2,1)} %param.7) | copy-start | bytes 6291460
  9.1 13.7 %all-to-all-start = ((s32[8,1,2]{2,1,0:T(1,128)}), s32[8,1,2]{2,1,0:T(1,128)S(1)}, u32[]{:S(2)}, u32[]{:S(2)}) async-start(s32[8,1,2]{2,1,0:T(1,128)} %bitcast.5), calls=%async_computation | async-start | bytes 8192 | tf_op jit(solution)/shard_map/all_to_all | solution.py:94
  22.3 6.2 %copy-start.1 = (bf16[2,16,1280]{2,1,0:T(8,128)(2,1)S(1)}, bf16[2,16,1280]{2,1,0:T(8,128)(2,1)}, u32[]{:S(2)}) copy-start(bf16[2,16,1280]{2,1,0:T(8,128)(2,1)} %param.6) | copy-start | bytes 245764
  22.3 6.3 %copy-start.3 = (bf16[2,2,16,256]{3,2,1,0:T(8,128)(2,1)S(1)}, bf16[2,2,16,256]{3,2,1,0:T(8,128)(2,1)}, u32[]{:S(2)}) copy-start(bf16[2,2,16,256]{3,2,1,0:T(8,128)(2,1)} %param.9) | copy-start | bytes 98308
  22.3 6.8 %copy-start.4 = (s32[2]{0:T(128)S(1)}, s32[2]{0:T(128)}, u32[]{:S(2)}) copy-start(s32[2]{0:T(128)} %param.10) | copy-start | bytes 28
  22.8 53.4 %all-to-all-start.1 = ((bf16[8,2,2,128,256]{3,4,1,2,0:T(8,128)(2,1)}), bf16[8,2,2,128,256]{3,4,1,2,0:T(8,128)(2,1)}, u32[]{:S(2)}, u32[]{:S(2)}) async-start(bf16[8,2,2,128,256]{3,4,1,2,0:T(8,128)(2,1)} %copy.89), calls=%async_computation.1 | async-start | bytes 4194304 | tf_op jit(solution)/shard_map/all_to_all | solution.py:93
  28.4 123.7 %reduce-scatter.4.cloned.1.call-start = ((), (), s32[]{:S(2)}) async-start(), calls=%async_computation.3 | async-start | bytes 73728
  81.5 1.9 %copy-start.2 = (bf16[1280,128]{1,0:T(8,128)(2,1)S(1)}, bf16[1280,128]{1,0:T(8,128)(2,1)}, u32[]{:S(2)}) copy-start(bf16[1280,128]{1,0:T(8,128)(2,1)} %param.11) | copy-start | bytes 983044
  89.5 63.9 %copy-start.5 = (f32[2]{0:T(128)}, f32[2]{0:T(128)S(1)}, u32[]{:S(2)}) copy-start(f32[2]{0:T(128)S(1)} %broadcast_multiply_fusion) | copy-start | bytes 28
Sparse Core Ops, SparseCore 0:
  90.6 61.5 reduce-scatter.3
